TPU v7x, 512 devices: a whole 4x8x8 slice. The times are simulated.
512 devices in a mesh: snap: 32 (over z, x_hi, core), space: 16 (over y, x_lo).
Axes of the slice: x: 4 (x_hi: 2, x_lo: 2; x = x_hi * 2 + x_lo), y: 8, z: 8, core: 2. Of those that a mesh axis runs over, the one named last changes fastest.
Arguments:
- snapshots: bfloat16 [65536, 4096], P('space', 'snap'), may hold values from -36 to 36
Outputs:
- gram_band: float32 [4096, 2176], P(('snap', 'space'))
- mean_field: float32 [65536], P('space')
All inputs are finite; a program needn't handle non-finite values.
Results may differ from a plain program's by a relative error of at most 0.00036.
Values may be sent and summed in bfloat16 or wider, within the bound.
A program may use at most 64 MiB of HBM per device.

v0:
```python
import jax
import jax.numpy as jnp
from jax import lax
from jax.sharding import PartitionSpec as P


def from_everyone(x, axis):
    copies = jnp.broadcast_to(x, (lax.axis_size(axis), *x.shape))
    return lax.all_to_all(copies, axis, split_axis=0, concat_axis=0, tiled=True)


def over_copies(x, axis):
    return from_everyone(x, axis).sum(axis=0)


def passed_along(x, axis, by):
    count = lax.axis_size(axis)
    return lax.ppermute(x, axis, [(i, (i + by) % count) for i in range(count)])


def split_up(x, dim, count):
    shape = x.shape
    blocks = x.reshape(*shape[:dim], count, shape[dim] // count, *shape[dim + 1 :])
    return jnp.moveaxis(blocks, dim, 0)


def summed_on_arrival(x, axis, dim):
    count = lax.axis_size(axis)
    blocks = lax.all_to_all(split_up(x, dim, count), axis, 0, 0, tiled=True)
    return jnp.sum(blocks, axis=0)


def cross_tiles(left_block, right_block):
    return lax.dot_general(
        left_block, right_block, (((0,), (0,)), ((), ())), preferred_element_type=jnp.float32
    )


def per_device(snapshots):
    snap_count = lax.axis_size("snap")
    space_count = lax.axis_size("space")
    row_count, block_width = snapshots.shape
    totals = jnp.sum(snapshots.astype(jnp.float32), axis=1)
    mean_field = over_copies(totals, "snap") / (block_width * snap_count)
    fluctuation = (snapshots.astype(jnp.float32) - mean_field[:, None]).astype(jnp.bfloat16)
    half_count = snap_count // 2
    pieces = [cross_tiles(fluctuation, fluctuation)]
    stride = 2 + 2 * (snap_count // 32)
    reach = half_count // stride
    offsets = list(range(1, stride)) + [stride * j for j in range(1, reach + 1)]
    held = {0: fluctuation}
    for offset in offsets:
        held[offset] = passed_along(fluctuation, "snap", -offset)
    by_offset = {}
    for lower in range(stride):
        group = jnp.concatenate(
            [cross_tiles(held[lower], held[stride * j]) for j in range(1, reach + 1)], axis=1
        )
        if lower > 0:
            group = passed_along(group, "snap", lower)
        for j in range(1, reach + 1):
            by_offset[stride * j - lower] = group[:, (j - 1) * block_width : j * block_width]
    for offset in range(1, half_count + 1):
        pieces.append(by_offset[offset])
    gram_band = jnp.concatenate(pieces, axis=1)
    gram_band = summed_on_arrival(gram_band, "space", 0)
    return (gram_band * (1.0 / (row_count * space_count)), mean_field)


def solution(mesh):
    return jax.shard_map(
        per_device,
        mesh=mesh,
        in_specs=(P("space", "snap"),),
        out_specs=(P(("snap", "space"), None), P("space")),
        check_vma=False,
    )
```

profile of v0, /device:TPU:1, one launch (start us, length us, event | category | flops | bytes accessed | tf_op | source)
XLA Modules:
  0.0 332.4 jit_solution(4707822888481492862)
XLA Ops:
  0.6 1.6 convert_reduce_fusion
  2.2 0.0 copy-start
  2.2 0.5 broadcast_in_dim.4
  2.7 31.1 %all_to_all.11 = f32[32,1,4096]{2,1,0:T(1,128)S(1)} all-to-all(f32[32,1,4096]{2,1,0:T(1,128)S(1)} %broadcast_in_dim.4), channel_id=1, replica_groups=mesh['snap'=32,'space'=16] {'snap'}, dimensions={0} | all-to-all | bytes 1048576 | tf_op jit(solution)/shard_map/all_to_all | solution.py:9
  33.8 0.4 reduce_sum.28
  34.1 0.0 copy-done
  34.1 0.0 copy-start.1
  34.2 0.7 fusion
  34.9 3.6 %collective-permute-start.6 = (bf16[4096,128]{1,0:T(8,128)(2,1)S(1)}, bf16[4096,128]{1,0:T(8,128)(2,1)S(1)}, u32[]{:S(2)}, u32[]{:S(2)}) collective-permute-start(bf16[4096,128]{1,0:T(8,128)(2,1)S(1)} %fusion), channel_id=1, source_target_pairs={{0,480},{16,496},{32,0},{48,16},{64,32},{80,48},{96,64},{112,80},{... | collective-permute-start | bytes 3145736 | tf_op jit(solution)/shard_map/ppermute | solution.py:18
  38.4 5.9 %collective-permute-start.4 = (bf16[4096,128]{1,0:T(8,128)(2,1)S(1)}, bf16[4096,128]{1,0:T(8,128)(2,1)S(1)}, u32[]{:S(2)}, u32[]{:S(2)}) collective-permute-start(bf16[4096,128]{1,0:T(8,128)(2,1)S(1)} %fusion), channel_id=1, source_target_pairs={{0,256},{16,272},{32,288},{48,304},{64,320},{80,336},{96,352},{112... | collective-permute-start | bytes 3145736 | tf_op jit(solution)/shard_map/ppermute | solution.py:18
  44.4 4.4 %collective-permute-start.3 = (bf16[4096,128]{1,0:T(8,128)(2,1)S(1)}, bf16[4096,128]{1,0:T(8,128)(2,1)S(1)}, u32[]{:S(2)}, u32[]{:S(2)}) collective-permute-start(bf16[4096,128]{1,0:T(8,128)(2,1)S(1)} %fusion), channel_id=1, source_target_pairs={{0,320},{16,336},{32,352},{48,368},{64,384},{80,400},{96,416},{112... | collective-permute-start | bytes 3145736 | tf_op jit(solution)/shard_map/ppermute | solution.py:18
  48.8 2.6 collective-permute-start.2
  51.4 1.9 collective-permute-start.1
  53.3 0.5 convolution_dynamic-update-slice_fusion.4
  53.8 0.0 copy-done.1
  53.8 8.0 %collective-permute-done.6 = bf16[4096,128]{1,0:T(8,128)(2,1)S(1)} collective-permute-done((bf16[4096,128]{1,0:T(8,128)(2,1)S(1)}, bf16[4096,128]{1,0:T(8,128)(2,1)S(1)}, u32[]{:S(2)}, u32[]{:S(2)}) %collective-permute-start.6) | collective-permute-done | bytes 1048608 | tf_op jit(solution)/shard_map/ppermute | solution.py:18
  61.9 3.9 %collective-permute-start.8 = (bf16[4096,128]{1,0:T(8,128)(2,1)S(1)}, bf16[4096,128]{1,0:T(8,128)(2,1)S(1)}, u32[]{:S(2)}, u32[]{:S(2)}) collective-permute-start(bf16[4096,128]{1,0:T(8,128)(2,1)S(1)} %fusion), channel_id=1, source_target_pairs={{0,496},{16,0},{32,16},{48,32},{64,48},{80,64},{96,80},{112,96},{1... | collective-permute-start | bytes 3145736 | tf_op jit(solution)/shard_map/ppermute | solution.py:18
  65.8 25.5 %collective-permute-done.4 = bf16[4096,128]{1,0:T(8,128)(2,1)S(1)} collective-permute-done((bf16[4096,128]{1,0:T(8,128)(2,1)S(1)}, bf16[4096,128]{1,0:T(8,128)(2,1)S(1)}, u32[]{:S(2)}, u32[]{:S(2)}) %collective-permute-start.4) | collective-permute-done | bytes 1048608 | tf_op jit(solution)/shard_map/ppermute | solution.py:18
  91.2 6.7 %collective-permute-start = (bf16[4096,128]{1,0:T(8,128)(2,1)S(1)}, bf16[4096,128]{1,0:T(8,128)(2,1)S(1)}, u32[]{:S(2)}, u32[]{:S(2)}) collective-permute-start(bf16[4096,128]{1,0:T(8,128)(2,1)S(1)} %fusion), channel_id=1, source_target_pairs={{0,464},{16,480},{32,496},{48,0},{64,16},{80,32},{96,48},{112,64},... | collective-permute-start | bytes 3145736 | tf_op jit(solution)/shard_map/ppermute | solution.py:18
  97.9 0.5 fusion.8
  98.4 74.5 %collective-permute-done.3 = bf16[4096,128]{1,0:T(8,128)(2,1)S(1)} collective-permute-done((bf16[4096,128]{1,0:T(8,128)(2,1)S(1)}, bf16[4096,128]{1,0:T(8,128)(2,1)S(1)}, u32[]{:S(2)}, u32[]{:S(2)}) %collective-permute-start.3) | collective-permute-done | bytes 1048608 | tf_op jit(solution)/shard_map/ppermute | solution.py:18
  172.9 0.5 fusion.7
  173.4 47.5 %collective-permute-done.2 = bf16[4096,128]{1,0:T(8,128)(2,1)S(1)} collective-permute-done((bf16[4096,128]{1,0:T(8,128)(2,1)S(1)}, bf16[4096,128]{1,0:T(8,128)(2,1)S(1)}, u32[]{:S(2)}, u32[]{:S(2)}) %collective-permute-start.2) | collective-permute-done | bytes 1048608 | tf_op jit(solution)/shard_map/ppermute | solution.py:18
  220.9 0.5 fusion.6
  221.4 21.1 %collective-permute-done.1 = bf16[4096,128]{1,0:T(8,128)(2,1)S(1)} collective-permute-done((bf16[4096,128]{1,0:T(8,128)(2,1)S(1)}, bf16[4096,128]{1,0:T(8,128)(2,1)S(1)}, u32[]{:S(2)}, u32[]{:S(2)}) %collective-permute-start.1) | collective-permute-done | bytes 1048608 | tf_op jit(solution)/shard_map/ppermute | solution.py:18
  242.5 0.5 fusion.5
  243.0 1.9 collective-permute-start.7
  244.9 32.8 %collective-permute-done = bf16[4096,128]{1,0:T(8,128)(2,1)S(1)} collective-permute-done((bf16[4096,128]{1,0:T(8,128)(2,1)S(1)}, bf16[4096,128]{1,0:T(8,128)(2,1)S(1)}, u32[]{:S(2)}, u32[]{:S(2)}) %collective-permute-start) | collective-permute-done | bytes 1048608 | tf_op jit(solution)/shard_map/ppermute | solution.py:18
  277.7 0.5 fusion.4
  278.1 0.5 fusion.3
  278.6 0.5 fusion.2
  279.1 0.5 fusion.1
  279.6 1.9 collective-permute-start.5
  281.5 0.0 collective-permute-done.8
  281.6 0.5 fusion.12
  282.0 0.5 fusion.11
  282.5 0.5 fusion.10
  283.0 0.5 fusion.9
  283.5 5.7 %collective-permute-start.9 = (f32[128,512]{0,1:T(8,128)S(1)}, f32[128,512]{0,1:T(8,128)S(1)}, u32[]{:S(2)}, u32[]{:S(2)}) collective-permute-start(f32[128,512]{0,1:T(8,128)S(1)} %pad_maximum_fusion.2), channel_id=1, source_target_pairs={{0,16},{16,32},{32,48},{48,64},{64,80},{80,96},{96,112},{112,128},... | collective-permute-start | bytes 786440 | tf_op jit(solution)/shard_map/ppermute | solution.py:18
  289.2 4.0 %collective-permute-done.5 = f32[128,512]{0,1:T(8,128)S(1)} collective-permute-done((f32[128,512]{0,1:T(8,128)S(1)}, f32[128,512]{0,1:T(8,128)S(1)}, u32[]{:S(2)}, u32[]{:S(2)}) %collective-permute-start.5) | collective-permute-done | bytes 262176 | tf_op jit(solution)/shard_map/ppermute | solution.py:18
  293.2 0.0 collective-permute-done.7
  293.2 0.0 collective-permute-done.9
  293.2 0.5 convolution_dynamic-update-slice_fusion.3
  293.8 0.5 convolution_dynamic-update-slice_fusion.2
  294.3 0.5 convolution_dynamic-update-slice_fusion.1
  294.8 0.5 convolution_dynamic-update-slice_fusion
  295.3 0.4 copy.6
  295.7 36.0 %all_to_all.12 = f32[16,8,2176]{2,1,0:T(8,128)S(1)} all-to-all(f32[16,8,2176]{2,1,0:T(8,128)S(1)} %bitcast.35), channel_id=1, replica_groups=mesh['snap'=32,'space'=16] {'space'}, dimensions={0} | all-to-all | bytes 2228224 | tf_op jit(solution)/shard_map/all_to_all | solution.py:29
  331.7 0.1 reduce_sum.29
  331.8 0.6 broadcast_multiply_fusion
  (16 shorter events, 0.2 us)
Async XLA Ops:
  2.2 31.9 %copy-start = (bf16[4096,128]{1,0:T(8,128)(2,1)S(1)}, bf16[4096,128]{1,0:T(8,128)(2,1)}, u32[]{:S(2)}) copy-start(bf16[4096,128]{1,0:T(8,128)(2,1)} %param.1) | copy-start | bytes 3145732
  34.1 19.7 %copy-start.1 = (f32[4096]{0:T(1024)}, f32[4096]{0:T(1024)S(1)}, u32[]{:S(2)}) copy-start(f32[4096]{0:T(1024)S(1)} %broadcast_multiply_fusion.1) | copy-start | bytes 49156
  34.9 27.0 %collective-permute-start.6 = (bf16[4096,128]{1,0:T(8,128)(2,1)S(1)}, bf16[4096,128]{1,0:T(8,128)(2,1)S(1)}, u32[]{:S(2)}, u32[]{:S(2)}) collective-permute-start(bf16[4096,128]{1,0:T(8,128)(2,1)S(1)} %fusion), channel_id=1, source_target_pairs={{0,480},{16,496},{32,0},{48,16},{64,32},{80,48},{96,64},{112,80},{... | collective-permute-start | bytes 3145736 | tf_op jit(solution)/shard_map/ppermute | solution.py:18
  38.4 52.8 %collective-permute-start.4 = (bf16[4096,128]{1,0:T(8,128)(2,1)S(1)}, bf16[4096,128]{1,0:T(8,128)(2,1)S(1)}, u32[]{:S(2)}, u32[]{:S(2)}) collective-permute-start(bf16[4096,128]{1,0:T(8,128)(2,1)S(1)} %fusion), channel_id=1, source_target_pairs={{0,256},{16,272},{32,288},{48,304},{64,320},{80,336},{96,352},{112... | collective-permute-start | bytes 3145736 | tf_op jit(solution)/shard_map/ppermute | solution.py:18
  44.4 128.5 %collective-permute-start.3 = (bf16[4096,128]{1,0:T(8,128)(2,1)S(1)}, bf16[4096,128]{1,0:T(8,128)(2,1)S(1)}, u32[]{:S(2)}, u32[]{:S(2)}) collective-permute-start(bf16[4096,128]{1,0:T(8,128)(2,1)S(1)} %fusion), channel_id=1, source_target_pairs={{0,320},{16,336},{32,352},{48,368},{64,384},{80,400},{96,416},{112... | collective-permute-start | bytes 3145736 | tf_op jit(solution)/shard_map/ppermute | solution.py:18
  48.8 172.1 %collective-permute-start.2 = (bf16[4096,128]{1,0:T(8,128)(2,1)S(1)}, bf16[4096,128]{1,0:T(8,128)(2,1)S(1)}, u32[]{:S(2)}, u32[]{:S(2)}) collective-permute-start(bf16[4096,128]{1,0:T(8,128)(2,1)S(1)} %fusion), channel_id=1, source_target_pairs={{0,384},{16,400},{32,416},{48,432},{64,448},{80,464},{96,480},{112... | collective-permute-start | bytes 3145736 | tf_op jit(solution)/shard_map/ppermute | solution.py:18
  51.4 191.1 %collective-permute-start.1 = (bf16[4096,128]{1,0:T(8,128)(2,1)S(1)}, bf16[4096,128]{1,0:T(8,128)(2,1)S(1)}, u32[]{:S(2)}, u32[]{:S(2)}) collective-permute-start(bf16[4096,128]{1,0:T(8,128)(2,1)S(1)} %fusion), channel_id=1, source_target_pairs={{0,448},{16,464},{32,480},{48,496},{64,0},{80,16},{96,32},{112,48}... | collective-permute-start | bytes 3145736 | tf_op jit(solution)/shard_map/ppermute | solution.py:18
  61.9 219.7 %collective-permute-start.8 = (bf16[4096,128]{1,0:T(8,128)(2,1)S(1)}, bf16[4096,128]{1,0:T(8,128)(2,1)S(1)}, u32[]{:S(2)}, u32[]{:S(2)}) collective-permute-start(bf16[4096,128]{1,0:T(8,128)(2,1)S(1)} %fusion), channel_id=1, source_target_pairs={{0,496},{16,0},{32,16},{48,32},{64,48},{80,64},{96,80},{112,96},{1... | collective-permute-start | bytes 3145736 | tf_op jit(solution)/shard_map/ppermute | solution.py:18
  91.2 186.5 %collective-permute-start = (bf16[4096,128]{1,0:T(8,128)(2,1)S(1)}, bf16[4096,128]{1,0:T(8,128)(2,1)S(1)}, u32[]{:S(2)}, u32[]{:S(2)}) collective-permute-start(bf16[4096,128]{1,0:T(8,128)(2,1)S(1)} %fusion), channel_id=1, source_target_pairs={{0,464},{16,480},{32,496},{48,0},{64,16},{80,32},{96,48},{112,64},... | collective-permute-start | bytes 3145736 | tf_op jit(solution)/shard_map/ppermute | solution.py:18
  243.0 50.2 %collective-permute-start.7 = (f32[128,512]{0,1:T(8,128)S(1)}, f32[128,512]{0,1:T(8,128)S(1)}, u32[]{:S(2)}, u32[]{:S(2)}) collective-permute-start(f32[128,512]{0,1:T(8,128)S(1)} %pad_maximum_fusion.1), channel_id=1, source_target_pairs={{0,32},{16,48},{32,64},{48,80},{64,96},{80,112},{96,128},{112,144}... | collective-permute-start | bytes 786440 | tf_op jit(solution)/shard_map/ppermute | solution.py:18
  279.6 13.6 %collective-permute-start.5 = (f32[128,512]{0,1:T(8,128)S(1)}, f32[128,512]{0,1:T(8,128)S(1)}, u32[]{:S(2)}, u32[]{:S(2)}) collective-permute-start(f32[128,512]{0,1:T(8,128)S(1)} %pad_maximum_fusion), channel_id=1, source_target_pairs={{0,48},{16,64},{32,80},{48,96},{64,112},{80,128},{96,144},{112,160... | collective-permute-start | bytes 786440 | tf_op jit(solution)/shard_map/ppermute | solution.py:18
  283.5 9.7 %collective-permute-start.9 = (f32[128,512]{0,1:T(8,128)S(1)}, f32[128,512]{0,1:T(8,128)S(1)}, u32[]{:S(2)}, u32[]{:S(2)}) collective-permute-start(f32[128,512]{0,1:T(8,128)S(1)} %pad_maximum_fusion.2), channel_id=1, source_target_pairs={{0,16},{16,32},{32,48},{48,64},{64,80},{80,96},{96,112},{112,128},... | collective-permute-start | bytes 786440 | tf_op jit(solution)/shard_map/ppermute | solution.py:18
where the time goes:
time: 333 us; the launch traced here: 332 us
  waiting for transfers between devices  213 us (64%)
  blocking collectives  67.1 us (20%)
  starting transfers between devices  38.5 us (12%)
  matrix products  8.13 us (2%)
  other arithmetic  3.4 us (1%)
    ppermute x10, waiting for transfers between devices, passed_along(): return lax.ppermute(x, axis, [(i, (i + by) % count) for i in range(count)])  213 us
    ppermute x10, starting transfers between devices, passed_along(): return lax.ppermute(x, axis, [(i, (i + by) % count) for i in range(count)])  38.5 us
    all_to_all x1, blocking collectives, summed_on_arrival(): blocks = lax.all_to_all(split_up(x, dim, count), axis, 0, 0, tiled=True)  36 us
    all_to_all x1, blocking collectives, from_everyone(): return lax.all_to_all(copies, axis, split_axis=0, concat_axis=0, tiled=True)  31.1 us
    dot_general x17, matrix products, cross_tiles(): lax.dot_general(left_block, right_block, (((0,), (0,)), ((), ())), prefer...  8.13 us
  transfers between devices with their start and end apart: 10, of which 7 were waited for; matrix products, arithmetic and copies ran while one was open for 2% of the time, Pallas kernels for 0%

commit v1 on v0

v1 whole, which is shorter than its diff:
```python
import jax
import jax.numpy as jnp
from jax import lax
from jax.experimental import pallas as pl
from jax.experimental.pallas import tpu as pltpu
from jax.sharding import PartitionSpec as P

MESH = pl.DeviceIdType.MESH
NZ, NX, NY = 8, 4, 8
LANES = 128
ROWS_Q = 1024
SNAPS = 4096
ROWS = 65536
GROUPS = 10
F32, BF16 = jnp.float32, jnp.bfloat16


def device(z, x, y, c):
    z, x, y = (z + NZ) % NZ, (x + NX) % NX, (y + NY) % NY
    return (z * 4 + (x // 2) * 2 + c, y * 2 + x % 2)


def wait_for(ref, sem):
    pltpu.make_async_copy(ref, ref, sem).wait()


def kernel(
    a_ref, gram_ref, mean_ref,
    raw0, lo1, hi1, lo2, hi2, lhs, mcol, psum, qrecv, zrecv, mall,
    part, drecv, xbuf, xrecv, ybuf, yrecv,
    quad_s, quad_r, psum_s, psum_r, zsum_s, zsum_r, mean_s, mean_r,
    up1_s, up1_r, dn1_s, dn1_r, up2_s, up2_r, dn2_s, dn2_r,
    d_s, d_r, x_s, x_r, y_s, y_r,
):
    s, p = lax.axis_index("snap"), lax.axis_index("space")
    z, xh, c = s // 4, (s // 2) % 2, s % 2
    y, xl = p // 2, p % 2
    x = xh * 2 + xl
    q0 = xh * 2 + c
    quad = {
        1: (device(z, x, y, 1 - c), xh * 2 + 1 - c),
        2: (device(z, x + 2, y, c), (1 - xh) * 2 + c),
        3: (device(z, x + 2, y, 1 - c), (1 - xh) * 2 + 1 - c),
    }

    def send(src, dst, ss, rs, to):
        pltpu.make_async_remote_copy(
            src_ref=src, dst_ref=dst, send_sem=ss, recv_sem=rs,
            device_id=to, device_id_type=MESH,
        ).start()

    barrier = pltpu.get_barrier_semaphore()
    sources = [device(z - k, x, y, c) for k in range(1, NZ)]
    sources += [quad[1][0], quad[2][0], quad[3][0]]
    sources += [device(z, x + 1, y, c), device(z, x + 3, y, c)]
    for shift in range(3):
        sources += [device(z + shift, x, y - k, c) for k in range(1, NY)]
    for to in sources:
        pl.semaphore_signal(barrier, inc=1, device_id=to, device_id_type=MESH)

    def row_sums(i, carry):
        block = a_ref[pl.ds(pl.multiple_of(i * LANES, LANES), LANES), :].astype(F32)
        psum[pl.ds(i, 1), :] = jnp.sum(block.T, axis=0, keepdims=True)
        return carry

    lax.fori_loop(0, 32, row_sums, 0)
    own_rows = pl.ds(pl.multiple_of(q0 * ROWS_Q, ROWS_Q), ROWS_Q)
    raw0[q0] = a_ref[own_rows, :]

    pl.semaphore_wait(barrier, len(sources))

    for j in (1, 2, 3):
        to, q = quad[j]
        send(psum.at[pl.ds(pl.multiple_of(q * 8, 8), 8)], qrecv.at[j - 1], psum_s, psum_r, to)

    above, below = device(z + 1, x, y, c), device(z - 1, x, y, c)

    def send_slab(src, a):
        send(src, lo1.at[a], up1_s.at[a], up1_r.at[a], above)
        send(src, hi1.at[a], dn1_s.at[a], dn1_r.at[a], below)

    send_slab(a_ref.at[own_rows], q0)
    for j in (1, 2, 3):
        to, q = quad[j]
        rows = pl.ds(pl.multiple_of(q * ROWS_Q, ROWS_Q), ROWS_Q)
        send(a_ref.at[rows], raw0.at[q0], quad_s.at[j - 1], quad_r.at[j - 1], to)

    wait_for(qrecv, psum_r)
    zrecv[z] = psum[pl.ds(pl.multiple_of(q0 * 8, 8), 8), :] + qrecv[0] + qrecv[1] + qrecv[2]
    for k in range(1, NZ):
        send(zrecv.at[z], zrecv.at[z], zsum_s, zsum_r, device(z + k, x, y, c))

    def quad_slab(j):
        q = quad[j][1]
        wait_for(raw0.at[q], quad_r.at[j - 1])
        send_slab(raw0.at[q], q)

    quad_slab(1)
    quad_slab(2)

    wait_for(zrecv.at[pl.ds(0, NZ - 1)], zsum_r)
    mean = zrecv[0]
    for k in range(1, NZ):
        mean = mean + zrecv[k]
    mean = mean * (1.0 / SNAPS)
    mall[q0] = mean
    for j in (1, 2, 3):
        send(mall.at[q0], mall.at[q0], mean_s, mean_r, quad[j][0])
    for g in range(8):
        mcol[pl.ds(g * LANES, LANES), :] = jnp.broadcast_to(mean[g : g + 1, :], (LANES, LANES)).T

    quad_slab(3)

    def centred(ref, a):
        return (ref[a].astype(F32) - mcol[...]).astype(BF16)

    def fill_lhs(ref, a, at):
        lhs[pl.ds(at * 512 + a * LANES, LANES), :] = centred(ref, a).T

    def store_unit(g, u, tile, first=0):
        blocks = tile.reshape((4 - first), 8, 2, 8, LANES)
        for a in range(4):
            for half in range(2):
                if a < first:
                    value = jnp.zeros((8, 8, LANES), F32)
                else:
                    value = blocks[a - first, :, half]
                part[g, a % 2, (a // 2) * 2 + half, u] = value

    def dot(start, size, right):
        return jnp.dot(lhs[pl.ds(start, size), :], right, preferred_element_type=F32)

    groups = [("a", 3), ("a", 1)] + [("b", t) for t in (3, 2, 1, 0)] + [("c", t) for t in (3, 2, 1, 0)]
    shifts = {"a": (0, 0), "b": (0, 1), "c": (1, 2)}
    dz = {"a": (0, 0), "b": (1, 2), "c": (3, 4)}

    def make(g):
        kind, t = groups[g]
        if kind == "a":
            for u in range(2):
                store_unit(g, u, dot(0, 512, centred(raw0, t - u)))
        elif kind == "b":
            right = centred(hi1, t)
            for u in range(2):
                store_unit(g, u, dot(u * 512, 512, right))
        else:
            wait_for(lo2.at[t], up2_r.at[t])
            wait_for(hi2.at[t], dn2_r.at[t])
            fill_lhs(lo2, t, 2)
            right = centred(hi2, t)
            store_unit(g, 0, dot(512, 512, right))
            store_unit(g, 1, dot(1024 + t * LANES, 512 - t * LANES, right), t)
        send(part.at[g, 1 - c], drecv.at[g], d_s.at[g], d_r.at[g], quad[1][0])

    def x_step(g):
        wait_for(drecv.at[g], d_r.at[g])
        xbuf[g] = part[g, c] + drecv[g]
        for k in range(1, NX):
            xt = (x + k) % NX
            send(xbuf.at[g, xt], xrecv.at[g, k - 1], x_s.at[g], x_r.at[g], device(z, xt, y, c))

    def y_step(g):
        wait_for(xrecv.at[g], x_r.at[g])
        ybuf[g] = xbuf[g, x] + xrecv[g, 0] + xrecv[g, 1] + xrecv[g, 2]
        for u in range(2):
            shift = shifts[groups[g][0]][u]
            for k in range(0 if shift else 1, NY):
                yt = (y + k) % NY
                send(ybuf.at[g, u, yt], yrecv.at[g, u, k], y_s.at[g, u], y_r.at[g, u], device(z - shift, x, yt, c))

    def o_step(g):
        kind, t = groups[g]
        for u in range(2):
            first = 0 if shifts[kind][u] else 1
            wait_for(yrecv.at[g, u, pl.ds(first, NY - first)], y_r.at[g, u])
            total = yrecv[g, u, 0] if first == 0 else ybuf[g, u, y]
            for k in range(1, NY):
                total = total + yrecv[g, u, k]
            total = total * (1.0 / ROWS)
            d = dz[kind][u]
            col = t - u if kind == "a" else t

            def put(total=total, d=d, col=col):
                at = pl.multiple_of((4 * d + col - q0) * LANES, LANES)
                gram_ref[:, pl.ds(at, LANES)] = total

            if d == 0:
                pl.when(col >= q0)(put)
            elif d == 4:
                pl.when(col <= q0)(put)
            else:
                put()

    for a in range(4):
        fill_lhs(raw0, a, 0)
    make(0)
    make(1)
    x_step(0)
    for t in (3, 2, 1, 0):
        wait_for(lo1.at[t], up1_r.at[t])
        send(lo1.at[t], lo2.at[t], up2_s.at[t], up2_r.at[t], above)
        wait_for(hi1.at[t], dn1_r.at[t])
        send(hi1.at[t], hi2.at[t], dn2_s.at[t], dn2_r.at[t], below)
    x_step(1)
    for t in (3, 2, 1, 0):
        fill_lhs(lo1, t, 1)
    for g in range(2, GROUPS):
        make(g)
        if g > 2:
            x_step(g - 1)
        y_step(g - 2)
        if g > 2:
            o_step(g - 3)
    x_step(GROUPS - 1)
    y_step(GROUPS - 2)
    o_step(GROUPS - 3)
    y_step(GROUPS - 1)
    o_step(GROUPS - 2)
    o_step(GROUPS - 1)

    wait_for(mall.at[pl.ds(0, 3)], mean_r)
    mean_ref[...] = mall[...]

    wait_for(qrecv, psum_s)
    wait_for(zrecv.at[pl.ds(0, NZ - 1)], zsum_s)
    wait_for(mall.at[pl.ds(0, 3)], mean_s)
    for j in range(3):
        wait_for(raw0.at[j], quad_s.at[j])
    for a in range(4):
        for sem in (up1_s, dn1_s, up2_s, dn2_s):
            wait_for(raw0.at[a], sem.at[a])
    for g in range(GROUPS):
        wait_for(drecv.at[g], d_s.at[g])
        wait_for(xrecv.at[g], x_s.at[g])
        for u in range(2):
            first = 0 if shifts[groups[g][0]][u] else 1
            wait_for(yrecv.at[g, u, pl.ds(first, NY - first)], y_s.at[g, u])


def per_device(snapshots):
    slab = lambda: pltpu.VMEM((4, ROWS_Q, LANES), BF16)
    dma = pltpu.SemaphoreType.DMA
    one = lambda: dma(())
    gram, mean = pl.pallas_call(
        kernel,
        out_shape=(
            jax.ShapeDtypeStruct((8, 17 * LANES), F32),
            jax.ShapeDtypeStruct((4, 8, LANES), F32),
        ),
        in_specs=[pl.BlockSpec(memory_space=pltpu.VMEM)],
        out_specs=(pl.BlockSpec(memory_space=pltpu.VMEM),) * 2,
        scratch_shapes=[
            slab(), slab(), slab(), slab(), slab(),
            pltpu.VMEM((3 * 512, ROWS_Q), BF16),
            pltpu.VMEM((ROWS_Q, LANES), F32),
            pltpu.VMEM((32, LANES), F32),
            pltpu.VMEM((3, 8, LANES), F32),
            pltpu.VMEM((NZ, 8, LANES), F32),
            pltpu.VMEM((4, 8, LANES), F32),
            pltpu.VMEM((GROUPS, 2, NX, 2, NY, 8, LANES), F32),
            pltpu.VMEM((GROUPS, NX, 2, NY, 8, LANES), F32),
            pltpu.VMEM((GROUPS, NX, 2, NY, 8, LANES), F32),
            pltpu.VMEM((GROUPS, NX - 1, 2, NY, 8, LANES), F32),
            pltpu.VMEM((GROUPS, 2, NY, 8, LANES), F32),
            pltpu.VMEM((GROUPS, 2, NY, 8, LANES), F32),
            dma((3,)), dma((3,)), one(), one(), one(), one(), one(), one(),
            dma((4,)), dma((4,)), dma((4,)), dma((4,)), dma((4,)), dma((4,)), dma((4,)), dma((4,)),
            dma((GROUPS,)), dma((GROUPS,)), dma((GROUPS,)), dma((GROUPS,)),
            dma((GROUPS, 2)), dma((GROUPS, 2)),
        ],
        compiler_params=pltpu.CompilerParams(
            collective_id=0, has_side_effects=True, vmem_limit_bytes=48 * 1024 * 1024
        ),
    )(snapshots)
    return gram, mean.reshape(-1)


def solution(mesh):
    return jax.shard_map(
        per_device,
        mesh=mesh,
        in_specs=(P("space", "snap"),),
        out_specs=(P(("snap", "space"), None), P("space")),
        check_vma=False,
    )
```

time: 333 us -> 93.1 us (0.28)
  waiting for transfers between devices: 213 us -> 0 us
  Pallas kernels: 0 us -> 89.6 us
  blocking collectives: 67.1 us -> 0 us
  starting transfers between devices: 38.5 us -> 0 us
  matrix products: 8.13 us -> 0 us
  other arithmetic: 3.4 us -> 0 us
    ppermute x10 -> x0, waiting for transfers between devices: 213 us -> none  [passed_along(): return lax.ppermute(x, axis, [(i, (i + by) % count) for i in range(count)])]
    pallas_call x0 -> x1, Pallas kernels: none -> 89.6 us  [per_device(): pl.pallas_call(kernel, out_shape=(jax.ShapeDtypeStruct((8, 17 * LANES), F...]
    all_to_all x2 -> x0, blocking collectives: 67.1 us -> none  [the longest x1 36 us: summed_on_arrival(): blocks = lax.all_to_all(split_up(x, dim, count), axis, 0, 0, tiled=True)]
    ppermute x10 -> x0, starting transfers between devices: 38.5 us -> none  [passed_along(): return lax.ppermute(x, axis, [(i, (i + by) % count) for i in range(count)])]
    dot_general x17 -> x0, matrix products: 8.13 us -> none  [cross_tiles(): lax.dot_general(left_block, right_block, (((0,), (0,)), ((), ())), prefer...]
  transfers between devices with their start and end apart: 10 -> 0, of which waited for: 7 -> 0; matrix products, arithmetic and copies ran while one was open for 2% -> 0% of each run, Pallas kernels for 0% -> 0%
where the time goes in v1:
time: 93.1 us; the launch traced here: 92.7 us
  Pallas kernels  89.6 us (96%)
  local copies, waits for them, and re-layouts  2.46 us (3%)
    pallas_call x1, Pallas kernels, per_device(): pl.pallas_call(kernel, out_shape=(jax.ShapeDtypeStruct((8, 17 * LANES), F...  89.6 us
    unnamed x4, local copies, waits for them, and re-layouts  2.46 us

profile of v1, /device:TPU:1, one launch (start us, length us, event | category | flops | bytes accessed | tf_op | source)
XLA Modules:
  0.0 92.7 jit_solution(6700844553156528780)
XLA Ops:
  0.6 0.0 copy-start
  0.6 1.2 %copy-done = bf16[4096,128]{1,0:T(8,128)(2,1)S(1)} copy-done((bf16[4096,128]{1,0:T(8,128)(2,1)S(1)}, bf16[4096,128]{1,0:T(8,128)(2,1)}, u32[]{:S(2)}) %copy-start) | copy-done | bytes 1048600
  1.9 89.6 %shard_map.30 = (f32[8,2176]{1,0:T(8,128)S(1)}, f32[4,8,128]{2,1,0:T(8,128)S(1)}) custom-call(bf16[4096,128]{1,0:T(8,128)(2,1)S(1)} %copy-done), custom_call_target="tpu_custom_call" | custom-call | tf_op jit(solution)/shard_map/pallas_call | solution.py:244
  91.5 0.6 copy.5
  92.1 0.6 copy.6
Async XLA Ops:
  0.6 1.2 %copy-start = (bf16[4096,128]{1,0:T(8,128)(2,1)S(1)}, bf16[4096,128]{1,0:T(8,128)(2,1)}, u32[]{:S(2)}) copy-start(bf16[4096,128]{1,0:T(8,128)(2,1)} %a_ref.1) | copy-start | bytes 3145732

commit v2 on v1

--- a/solution.py
+++ b/solution.py
@@ -27,10 +27,10 @@
 def kernel(
     a_ref, gram_ref, mean_ref,
     raw0, lo1, hi1, lo2, hi2, lhs, mcol, psum, qrecv, zrecv, mall,
-    part, drecv, xbuf, xrecv, ybuf, yrecv,
+    part, drecv, xbuf, xrecv, ybuf, yrecv, obuf, orecv,
     quad_s, quad_r, psum_s, psum_r, zsum_s, zsum_r, mean_s, mean_r,
     up1_s, up1_r, dn1_s, dn1_r, up2_s, up2_r, dn2_s, dn2_r,
-    d_s, d_r, x_s, x_r, y_s, y_r,
+    d_s, d_r, x_s, x_r, y_s, y_r, o_s, o_r, token, complete,
 ):
     s, p = lax.axis_index("snap"), lax.axis_index("space")
     z, xh, c = s // 4, (s // 2) % 2, s % 2
@@ -50,13 +50,17 @@
         ).start()
 
     barrier = pltpu.get_barrier_semaphore()
-    sources = [device(z - k, x, y, c) for k in range(1, NZ)]
-    sources += [quad[1][0], quad[2][0], quad[3][0]]
-    sources += [device(z, x + 1, y, c), device(z, x + 3, y, c)]
-    for shift in range(3):
-        sources += [device(z + shift, x, y - k, c) for k in range(1, NY)]
-    for to in sources:
-        pl.semaphore_signal(barrier, inc=1, device_id=to, device_id_type=MESH)
+
+    def tell(sem, to):
+        pl.semaphore_signal(sem, inc=1, device_id=to, device_id_type=MESH)
+
+    above, below = device(z + 1, x, y, c), device(z - 1, x, y, c)
+    partners = [quad[1][0], quad[2][0], quad[3][0]]
+    partners += [device(z, x + 1, y, c), device(z, x + 3, y, c)]
+    partners += [device(z, x, y - k, c) for k in range(1, NY)]
+    for to in partners + [below]:
+        tell(barrier, to)
+    pl.when(z != NZ - 1)(lambda: tell(barrier, above))
 
     def row_sums(i, carry):
         block = a_ref[pl.ds(pl.multiple_of(i * LANES, LANES), LANES), :].astype(F32)
@@ -67,35 +71,60 @@
     own_rows = pl.ds(pl.multiple_of(q0 * ROWS_Q, ROWS_Q), ROWS_Q)
     raw0[q0] = a_ref[own_rows, :]
 
-    pl.semaphore_wait(barrier, len(sources))
+    pl.semaphore_wait(barrier, len(partners) + 1 + (z + NZ - 1) // NZ)
 
     for j in (1, 2, 3):
         to, q = quad[j]
         send(psum.at[pl.ds(pl.multiple_of(q * 8, 8), 8)], qrecv.at[j - 1], psum_s, psum_r, to)
 
-    above, below = device(z + 1, x, y, c), device(z - 1, x, y, c)
-
-    def send_slab(src, a):
+    def send_up(src, a):
         send(src, lo1.at[a], up1_s.at[a], up1_r.at[a], above)
+
+    def send_down(src, a):
         send(src, hi1.at[a], dn1_s.at[a], dn1_r.at[a], below)
 
-    send_slab(a_ref.at[own_rows], q0)
+    send_up(a_ref.at[own_rows], q0)
+    pl.when(z != 0)(lambda: send_down(a_ref.at[own_rows], q0))
     for j in (1, 2, 3):
         to, q = quad[j]
         rows = pl.ds(pl.multiple_of(q * ROWS_Q, ROWS_Q), ROWS_Q)
         send(a_ref.at[rows], raw0.at[q0], quad_s.at[j - 1], quad_r.at[j - 1], to)
 
+    pl.when(z != 0)(lambda: pl.semaphore_wait(token, 1))
+    pl.when(z != NZ - 1)(lambda: tell(token, above))
+
+    @pl.when(z == NZ - 1)
+    def _():
+        for k in range(1, NZ):
+            tell(complete, device(z + k, x, y, c))
+
     wait_for(qrecv, psum_r)
     zrecv[z] = psum[pl.ds(pl.multiple_of(q0 * 8, 8), 8), :] + qrecv[0] + qrecv[1] + qrecv[2]
-    for k in range(1, NZ):
-        send(zrecv.at[z], zrecv.at[z], zsum_s, zsum_r, device(z + k, x, y, c))
+
+    def sums_along_z():
+        pl.when(z != NZ - 1)(lambda: pl.semaphore_wait(complete, 1))
+        for k in range(1, NZ):
+            send(zrecv.at[z], zrecv.at[z], zsum_s, zsum_r, device(z + k, x, y, c))
+
+    sibling = quad[1][1]
+    pl.when(z >= 3)(sums_along_z)
+    wait_for(raw0.at[sibling], quad_r.at[0])
+    send_up(raw0.at[sibling], sibling)
+
+    @pl.when(z < 3)
+    def _():
+        pl.when(z != 0)(lambda: send_down(raw0.at[sibling], sibling))
+        sums_along_z()
+        pl.when(z == 0)(lambda: send_down(a_ref.at[own_rows], q0))
+
+    pl.when((z == 0) | (z >= 3))(lambda: send_down(raw0.at[sibling], sibling))
 
     def quad_slab(j):
         q = quad[j][1]
         wait_for(raw0.at[q], quad_r.at[j - 1])
-        send_slab(raw0.at[q], q)
-
-    quad_slab(1)
+        send_up(raw0.at[q], q)
+        send_down(raw0.at[q], q)
+
     quad_slab(2)
 
     wait_for(zrecv.at[pl.ds(0, NZ - 1)], zsum_r)
@@ -125,7 +154,7 @@
                     value = jnp.zeros((8, 8, LANES), F32)
                 else:
                     value = blocks[a - first, :, half]
-                part[g, a % 2, (a // 2) * 2 + half, u] = value
+                part[g, a % 2, (a // 2) * 2 + half, :, u] = value
 
     def dot(start, size, right):
         return jnp.dot(lhs[pl.ds(start, size), :], right, preferred_element_type=F32)
@@ -162,21 +191,29 @@
     def y_step(g):
         wait_for(xrecv.at[g], x_r.at[g])
         ybuf[g] = xbuf[g, x] + xrecv[g, 0] + xrecv[g, 1] + xrecv[g, 2]
+        for k in range(1, NY):
+            yt = (y + k) % NY
+            send(ybuf.at[g, yt], yrecv.at[g, k - 1], y_s.at[g], y_r.at[g], device(z, x, yt, c))
+
+    def o_step(g):
+        wait_for(yrecv.at[g], y_r.at[g])
+        total = ybuf[g, y]
+        for k in range(NY - 1):
+            total = total + yrecv[g, k]
+        obuf[g] = total * (1.0 / ROWS)
         for u in range(2):
             shift = shifts[groups[g][0]][u]
-            for k in range(0 if shift else 1, NY):
-                yt = (y + k) % NY
-                send(ybuf.at[g, u, yt], yrecv.at[g, u, k], y_s.at[g, u], y_r.at[g, u], device(z - shift, x, yt, c))
-
-    def o_step(g):
+            if shift:
+                send(obuf.at[g, u], orecv.at[g, u], o_s.at[g, u], o_r.at[g, u], device(z - shift, x, y, c))
+
+    def f_step(g):
         kind, t = groups[g]
         for u in range(2):
-            first = 0 if shifts[kind][u] else 1
-            wait_for(yrecv.at[g, u, pl.ds(first, NY - first)], y_r.at[g, u])
-            total = yrecv[g, u, 0] if first == 0 else ybuf[g, u, y]
-            for k in range(1, NY):
-                total = total + yrecv[g, u, k]
-            total = total * (1.0 / ROWS)
+            if shifts[kind][u]:
+                wait_for(orecv.at[g, u], o_r.at[g, u])
+                total = orecv[g, u]
+            else:
+                total = obuf[g, u]
             d = dz[kind][u]
             col = t - u if kind == "a" else t
 
@@ -204,19 +241,18 @@
     x_step(1)
     for t in (3, 2, 1, 0):
         fill_lhs(lo1, t, 1)
-    for g in range(2, GROUPS):
-        make(g)
-        if g > 2:
-            x_step(g - 1)
-        y_step(g - 2)
-        if g > 2:
-            o_step(g - 3)
-    x_step(GROUPS - 1)
-    y_step(GROUPS - 2)
-    o_step(GROUPS - 3)
-    y_step(GROUPS - 1)
-    o_step(GROUPS - 2)
-    o_step(GROUPS - 1)
+    steps = {"m": make, "x": x_step, "y": y_step, "o": o_step}
+    order = (
+        ("m", 2), ("m", 3), ("x", 2), ("m", 4), ("x", 3), ("m", 5), ("x", 4), ("y", 0), ("x", 5), ("y", 1), ("o", 0),
+        ("m", 6), ("x", 6), ("y", 2), ("o", 1), ("y", 3),
+        ("m", 7), ("x", 7), ("y", 4), ("o", 2), ("y", 5), ("o", 3),
+        ("m", 8), ("x", 8), ("y", 6), ("o", 4), ("o", 5), ("y", 7), ("o", 6),
+        ("m", 9), ("y", 8), ("x", 9), ("o", 7), ("o", 8), ("y", 9), ("o", 9),
+    )
+    for kind, g in order:
+        steps[kind](g)
+    for g in range(GROUPS):
+        f_step(g)
 
     wait_for(mall.at[pl.ds(0, 3)], mean_r)
     mean_ref[...] = mall[...]
@@ -232,9 +268,10 @@
     for g in range(GROUPS):
         wait_for(drecv.at[g], d_s.at[g])
         wait_for(xrecv.at[g], x_s.at[g])
+        wait_for(yrecv.at[g], y_s.at[g])
         for u in range(2):
-            first = 0 if shifts[groups[g][0]][u] else 1
-            wait_for(yrecv.at[g, u, pl.ds(first, NY - first)], y_s.at[g, u])
+            if shifts[groups[g][0]][u]:
+                wait_for(orecv.at[g, u], o_s.at[g, u])
 
 
 def per_device(snapshots):
@@ -257,16 +294,19 @@
             pltpu.VMEM((3, 8, LANES), F32),
             pltpu.VMEM((NZ, 8, LANES), F32),
             pltpu.VMEM((4, 8, LANES), F32),
-            pltpu.VMEM((GROUPS, 2, NX, 2, NY, 8, LANES), F32),
-            pltpu.VMEM((GROUPS, NX, 2, NY, 8, LANES), F32),
-            pltpu.VMEM((GROUPS, NX, 2, NY, 8, LANES), F32),
-            pltpu.VMEM((GROUPS, NX - 1, 2, NY, 8, LANES), F32),
-            pltpu.VMEM((GROUPS, 2, NY, 8, LANES), F32),
-            pltpu.VMEM((GROUPS, 2, NY, 8, LANES), F32),
+            pltpu.VMEM((GROUPS, 2, NX, NY, 2, 8, LANES), F32),
+            pltpu.VMEM((GROUPS, NX, NY, 2, 8, LANES), F32),
+            pltpu.VMEM((GROUPS, NX, NY, 2, 8, LANES), F32),
+            pltpu.VMEM((GROUPS, NX - 1, NY, 2, 8, LANES), F32),
+            pltpu.VMEM((GROUPS, NY, 2, 8, LANES), F32),
+            pltpu.VMEM((GROUPS, NY - 1, 2, 8, LANES), F32),
+            pltpu.VMEM((GROUPS, 2, 8, LANES), F32),
+            pltpu.VMEM((GROUPS, 2, 8, LANES), F32),
             dma((3,)), dma((3,)), one(), one(), one(), one(), one(), one(),
             dma((4,)), dma((4,)), dma((4,)), dma((4,)), dma((4,)), dma((4,)), dma((4,)), dma((4,)),
             dma((GROUPS,)), dma((GROUPS,)), dma((GROUPS,)), dma((GROUPS,)),
-            dma((GROUPS, 2)), dma((GROUPS, 2)),
+            dma((GROUPS,)), dma((GROUPS,)), dma((GROUPS, 2)), dma((GROUPS, 2)),
+            pltpu.SemaphoreType.REGULAR, pltpu.SemaphoreType.REGULAR,
         ],
         compiler_params=pltpu.CompilerParams(
             collective_id=0, has_side_effects=True, vmem_limit_bytes=48 * 1024 * 1024

time: 93.1 us -> 83.9 us (0.901)
  Pallas kernels: 89.6 us -> 80.6 us
    pallas_call x1, Pallas kernels: 89.6 us -> 80.6 us  [per_device(): pl.pallas_call(kernel, out_shape=(jax.ShapeDtypeStruct((8, 17 * LANES), F...]
where the time goes in v2:
time: 83.9 us; the launch traced here: 83.7 us
  Pallas kernels  80.6 us (96%)
  local copies, waits for them, and re-layouts  2.46 us (3%)
    pallas_call x1, Pallas kernels, per_device(): pl.pallas_call(kernel, out_shape=(jax.ShapeDtypeStruct((8, 17 * LANES), F...  80.6 us
    unnamed x4, local copies, waits for them, and re-layouts  2.46 us

profile of v2, /device:TPU:1, one launch (start us, length us, event | category | flops | bytes accessed | tf_op | source)
XLA Modules:
  0.0 83.7 jit_solution(14698558334086374053)
XLA Ops:
  0.6 0.0 copy-start
  0.6 1.2 %copy-done = bf16[4096,128]{1,0:T(8,128)(2,1)S(1)} copy-done((bf16[4096,128]{1,0:T(8,128)(2,1)S(1)}, bf16[4096,128]{1,0:T(8,128)(2,1)}, u32[]{:S(2)}) %copy-start) | copy-done | bytes 1048600
  1.9 80.6 %shard_map.30 = (f32[8,2176]{1,0:T(8,128)S(1)}, f32[4,8,128]{2,1,0:T(8,128)S(1)}) custom-call(bf16[4096,128]{1,0:T(8,128)(2,1)S(1)} %copy-done), custom_call_target="tpu_custom_call" | custom-call | tf_op jit(solution)/shard_map/pallas_call | solution.py:281
  82.5 0.6 copy.5
  83.1 0.6 copy.6
Async XLA Ops:
  0.6 1.2 %copy-start = (bf16[4096,128]{1,0:T(8,128)(2,1)S(1)}, bf16[4096,128]{1,0:T(8,128)(2,1)}, u32[]{:S(2)}) copy-start(bf16[4096,128]{1,0:T(8,128)(2,1)} %a_ref.1) | copy-start | bytes 3145732

commit v3 on v2

--- a/solution.py
+++ b/solution.py
@@ -154,7 +154,7 @@
                     value = jnp.zeros((8, 8, LANES), F32)
                 else:
                     value = blocks[a - first, :, half]
-                part[g, a % 2, (a // 2) * 2 + half, :, u] = value
+                part[g, u, a % 2, (a // 2) * 2 + half] = value
 
     def dot(start, size, right):
         return jnp.dot(lhs[pl.ds(start, size), :], right, preferred_element_type=F32)
@@ -162,36 +162,44 @@
     groups = [("a", 3), ("a", 1)] + [("b", t) for t in (3, 2, 1, 0)] + [("c", t) for t in (3, 2, 1, 0)]
     shifts = {"a": (0, 0), "b": (0, 1), "c": (1, 2)}
     dz = {"a": (0, 0), "b": (1, 2), "c": (3, 4)}
+
+    def swap(g, u):
+        send(part.at[g, u, 1 - c], drecv.at[g, u], d_s.at[g, u], d_r.at[g, u], quad[1][0])
 
     def make(g):
         kind, t = groups[g]
         if kind == "a":
             for u in range(2):
                 store_unit(g, u, dot(0, 512, centred(raw0, t - u)))
+                swap(g, u)
         elif kind == "b":
             right = centred(hi1, t)
             for u in range(2):
                 store_unit(g, u, dot(u * 512, 512, right))
+                swap(g, u)
         else:
-            wait_for(lo2.at[t], up2_r.at[t])
             wait_for(hi2.at[t], dn2_r.at[t])
-            fill_lhs(lo2, t, 2)
             right = centred(hi2, t)
             store_unit(g, 0, dot(512, 512, right))
+            swap(g, 0)
+            wait_for(lo2.at[t], up2_r.at[t])
+            fill_lhs(lo2, t, 2)
             store_unit(g, 1, dot(1024 + t * LANES, 512 - t * LANES, right), t)
-        send(part.at[g, 1 - c], drecv.at[g], d_s.at[g], d_r.at[g], quad[1][0])
+            swap(g, 1)
 
     def x_step(g):
-        wait_for(drecv.at[g], d_r.at[g])
-        xbuf[g] = part[g, c] + drecv[g]
-        for k in range(1, NX):
-            xt = (x + k) % NX
-            send(xbuf.at[g, xt], xrecv.at[g, k - 1], x_s.at[g], x_r.at[g], device(z, xt, y, c))
+        for u in range(2):
+            wait_for(drecv.at[g, u], d_r.at[g, u])
+            xbuf[g, u] = part[g, u, c] + drecv[g, u]
+            for k in (2, 1, 3):
+                xt = (x + k) % NX
+                send(xbuf.at[g, u, xt], xrecv.at[g, u, k - 1], x_s.at[g, u], x_r.at[g, u], device(z, xt, y, c))
 
     def y_step(g):
-        wait_for(xrecv.at[g], x_r.at[g])
-        ybuf[g] = xbuf[g, x] + xrecv[g, 0] + xrecv[g, 1] + xrecv[g, 2]
-        for k in range(1, NY):
+        for u in range(2):
+            wait_for(xrecv.at[g, u], x_r.at[g, u])
+            ybuf[g, :, u] = xbuf[g, u, x] + xrecv[g, u, 0] + xrecv[g, u, 1] + xrecv[g, u, 2]
+        for k in (4, 3, 5, 2, 6, 1, 7):
             yt = (y + k) % NY
             send(ybuf.at[g, yt], yrecv.at[g, k - 1], y_s.at[g], y_r.at[g], device(z, x, yt, c))
 
@@ -242,13 +250,7 @@
     for t in (3, 2, 1, 0):
         fill_lhs(lo1, t, 1)
     steps = {"m": make, "x": x_step, "y": y_step, "o": o_step}
-    order = (
-        ("m", 2), ("m", 3), ("x", 2), ("m", 4), ("x", 3), ("m", 5), ("x", 4), ("y", 0), ("x", 5), ("y", 1), ("o", 0),
-        ("m", 6), ("x", 6), ("y", 2), ("o", 1), ("y", 3),
-        ("m", 7), ("x", 7), ("y", 4), ("o", 2), ("y", 5), ("o", 3),
-        ("m", 8), ("x", 8), ("y", 6), ("o", 4), ("o", 5), ("y", 7), ("o", 6),
-        ("m", 9), ("y", 8), ("x", 9), ("o", 7), ("o", 8), ("y", 9), ("o", 9),
-    )
+    order = (("m", 2), ("m", 3), ("x", 2), ("m", 4), ("x", 3), ("m", 5), ("x", 4), ("x", 5), ("y", 0), ("y", 1), ("m", 6), ("x", 6), ("o", 0), ("y", 2), ("o", 1), ("m", 7), ("x", 7), ("y", 3), ("y", 4), ("o", 2), ("m", 8), ("x", 8), ("y", 5), ("y", 6), ("o", 3), ("o", 4), ("m", 9), ("x", 9), ("y", 7), ("y", 8), ("o", 5), ("o", 6), ("o", 7), ("o", 8), ("y", 9), ("o", 9),)
     for kind, g in order:
         steps[kind](g)
     for g in range(GROUPS):
@@ -266,10 +268,10 @@
         for sem in (up1_s, dn1_s, up2_s, dn2_s):
             wait_for(raw0.at[a], sem.at[a])
     for g in range(GROUPS):
-        wait_for(drecv.at[g], d_s.at[g])
-        wait_for(xrecv.at[g], x_s.at[g])
         wait_for(yrecv.at[g], y_s.at[g])
         for u in range(2):
+            wait_for(drecv.at[g, u], d_s.at[g, u])
+            wait_for(xrecv.at[g, u], x_s.at[g, u])
             if shifts[groups[g][0]][u]:
                 wait_for(orecv.at[g, u], o_s.at[g, u])
 
@@ -294,17 +296,17 @@
             pltpu.VMEM((3, 8, LANES), F32),
             pltpu.VMEM((NZ, 8, LANES), F32),
             pltpu.VMEM((4, 8, LANES), F32),
-            pltpu.VMEM((GROUPS, 2, NX, NY, 2, 8, LANES), F32),
-            pltpu.VMEM((GROUPS, NX, NY, 2, 8, LANES), F32),
-            pltpu.VMEM((GROUPS, NX, NY, 2, 8, LANES), F32),
-            pltpu.VMEM((GROUPS, NX - 1, NY, 2, 8, LANES), F32),
+            pltpu.VMEM((GROUPS, 2, 2, NX, NY, 8, LANES), F32),
+            pltpu.VMEM((GROUPS, 2, NX, NY, 8, LANES), F32),
+            pltpu.VMEM((GROUPS, 2, NX, NY, 8, LANES), F32),
+            pltpu.VMEM((GROUPS, 2, NX - 1, NY, 8, LANES), F32),
             pltpu.VMEM((GROUPS, NY, 2, 8, LANES), F32),
             pltpu.VMEM((GROUPS, NY - 1, 2, 8, LANES), F32),
             pltpu.VMEM((GROUPS, 2, 8, LANES), F32),
             pltpu.VMEM((GROUPS, 2, 8, LANES), F32),
             dma((3,)), dma((3,)), one(), one(), one(), one(), one(), one(),
             dma((4,)), dma((4,)), dma((4,)), dma((4,)), dma((4,)), dma((4,)), dma((4,)), dma((4,)),
-            dma((GROUPS,)), dma((GROUPS,)), dma((GROUPS,)), dma((GROUPS,)),
+            dma((GROUPS, 2)), dma((GROUPS, 2)), dma((GROUPS, 2)), dma((GROUPS, 2)),
             dma((GROUPS,)), dma((GROUPS,)), dma((GROUPS, 2)), dma((GROUPS, 2)),
             pltpu.SemaphoreType.REGULAR, pltpu.SemaphoreType.REGULAR,
         ],

time: 83.9 us -> 82.5 us (0.983)
  the two profiles are of different devices: /device:TPU:1 before, /device:TPU:2 now
where the time goes in v3:
time: 82.5 us; the launch traced here: 82.4 us
  Pallas kernels  79.3 us (96%)
  local copies, waits for them, and re-layouts  2.46 us (3%)
    pallas_call x1, Pallas kernels, per_device(): pl.pallas_call(kernel, out_shape=(jax.ShapeDtypeStruct((8, 17 * LANES), F...  79.3 us
    unnamed x4, local copies, waits for them, and re-layouts  2.46 us

profile of v3, /device:TPU:2, one launch (start us, length us, event | category | flops | bytes accessed | tf_op | source)
XLA Modules:
  0.0 82.4 jit_solution(12661306367347278012)
XLA Ops:
  0.6 0.0 copy-start
  0.6 1.2 %copy-done = bf16[4096,128]{1,0:T(8,128)(2,1)S(1)} copy-done((bf16[4096,128]{1,0:T(8,128)(2,1)S(1)}, bf16[4096,128]{1,0:T(8,128)(2,1)}, u32[]{:S(2)}) %copy-start) | copy-done | bytes 1048600
  1.9 79.3 %shard_map.30 = (f32[8,2176]{1,0:T(8,128)S(1)}, f32[4,8,128]{2,1,0:T(8,128)S(1)}) custom-call(bf16[4096,128]{1,0:T(8,128)(2,1)S(1)} %copy-done), custom_call_target="tpu_custom_call" | custom-call | tf_op jit(solution)/shard_map/pallas_call | solution.py:283
  81.1 0.6 copy.5
  81.8 0.6 copy.6
Async XLA Ops:
  0.6 1.2 %copy-start = (bf16[4096,128]{1,0:T(8,128)(2,1)S(1)}, bf16[4096,128]{1,0:T(8,128)(2,1)}, u32[]{:S(2)}) copy-start(bf16[4096,128]{1,0:T(8,128)(2,1)} %a_ref.1) | copy-start | bytes 3145732

commit v4 on v3

--- a/solution.py
+++ b/solution.py
@@ -187,18 +187,39 @@
             store_unit(g, 1, dot(1024 + t * LANES, 512 - t * LANES, right), t)
             swap(g, 1)
 
+    def where_used(g, u, a, run):
+        kind, t = groups[g]
+        col = t - u if kind == "a" else t
+        if dz[kind][u] == 0 and col < 3:
+            pl.when(a <= col)(run)
+        elif dz[kind][u] == 4 and col > 0:
+            pl.when(a >= col)(run)
+        else:
+            run()
+
     def x_step(g):
         for u in range(2):
             wait_for(drecv.at[g, u], d_r.at[g, u])
             xbuf[g, u] = part[g, u, c] + drecv[g, u]
             for k in (2, 1, 3):
                 xt = (x + k) % NX
-                send(xbuf.at[g, u, xt], xrecv.at[g, u, k - 1], x_s.at[g, u], x_r.at[g, u], device(z, xt, y, c))
+
+                def go(k=k, xt=xt, u=u):
+                    send(
+                        xbuf.at[g, u, xt], xrecv.at[g, u, k - 1],
+                        x_s.at[g, u, k - 1], x_r.at[g, u], device(z, xt, y, c),
+                    )
+
+                where_used(g, u, (xt // 2) * 2 + c, go)
 
     def y_step(g):
         for u in range(2):
-            wait_for(xrecv.at[g, u], x_r.at[g, u])
-            ybuf[g, :, u] = xbuf[g, u, x] + xrecv[g, u, 0] + xrecv[g, u, 1] + xrecv[g, u, 2]
+
+            def add(u=u):
+                wait_for(xrecv.at[g, u], x_r.at[g, u])
+                ybuf[g, :, u] = xbuf[g, u, x] + xrecv[g, u, 0] + xrecv[g, u, 1] + xrecv[g, u, 2]
+
+            where_used(g, u, q0, add)
         for k in (4, 3, 5, 2, 6, 1, 7):
             yt = (y + k) % NY
             send(ybuf.at[g, yt], yrecv.at[g, k - 1], y_s.at[g], y_r.at[g], device(z, x, yt, c))
@@ -271,7 +292,9 @@
         wait_for(yrecv.at[g], y_s.at[g])
         for u in range(2):
             wait_for(drecv.at[g, u], d_s.at[g, u])
-            wait_for(xrecv.at[g, u], x_s.at[g, u])
+            for k in range(1, NX):
+                left = lambda: wait_for(xrecv.at[g, u, 0], x_s.at[g, u, k - 1])
+                where_used(g, u, (((x + k) % NX) // 2) * 2 + c, left)
             if shifts[groups[g][0]][u]:
                 wait_for(orecv.at[g, u], o_s.at[g, u])
 
@@ -306,7 +329,7 @@
             pltpu.VMEM((GROUPS, 2, 8, LANES), F32),
             dma((3,)), dma((3,)), one(), one(), one(), one(), one(), one(),
             dma((4,)), dma((4,)), dma((4,)), dma((4,)), dma((4,)), dma((4,)), dma((4,)), dma((4,)),
-            dma((GROUPS, 2)), dma((GROUPS, 2)), dma((GROUPS, 2)), dma((GROUPS, 2)),
+            dma((GROUPS, 2)), dma((GROUPS, 2)), dma((GROUPS, 2, NX - 1)), dma((GROUPS, 2)),
             dma((GROUPS,)), dma((GROUPS,)), dma((GROUPS, 2)), dma((GROUPS, 2)),
             pltpu.SemaphoreType.REGULAR, pltpu.SemaphoreType.REGULAR,
         ],

time: 82.5 us -> 82.9 us (level)
  the two profiles are of different devices: /device:TPU:2 before, /device:TPU:1 now
where the time goes in v4:
time: 82.9 us; the launch traced here: 81.5 us
  Pallas kernels  78.4 us (95%)
  local copies, waits for them, and re-layouts  2.46 us (3%)
    pallas_call x1, Pallas kernels, per_device(): pl.pallas_call(kernel, out_shape=(jax.ShapeDtypeStruct((8, 17 * LANES), F...  78.4 us
    unnamed x4, local copies, waits for them, and re-layouts  2.46 us

profile of v4, /device:TPU:1, one launch (start us, length us, event | category | flops | bytes accessed | tf_op | source)
XLA Modules:
  0.0 81.5 jit_solution(2105418070028694859)
XLA Ops:
  0.6 0.0 copy-start
  0.6 1.2 %copy-done = bf16[4096,128]{1,0:T(8,128)(2,1)S(1)} copy-done((bf16[4096,128]{1,0:T(8,128)(2,1)S(1)}, bf16[4096,128]{1,0:T(8,128)(2,1)}, u32[]{:S(2)}) %copy-start) | copy-done | bytes 1048600
  1.9 78.4 %shard_map.30 = (f32[8,2176]{1,0:T(8,128)S(1)}, f32[4,8,128]{2,1,0:T(8,128)S(1)}) custom-call(bf16[4096,128]{1,0:T(8,128)(2,1)S(1)} %copy-done), custom_call_target="tpu_custom_call" | custom-call | tf_op jit(solution)/shard_map/pallas_call | solution.py:306
  80.2 0.6 copy.5
  80.9 0.6 copy.6
Async XLA Ops:
  0.6 1.2 %copy-start = (bf16[4096,128]{1,0:T(8,128)(2,1)S(1)}, bf16[4096,128]{1,0:T(8,128)(2,1)}, u32[]{:S(2)}) copy-start(bf16[4096,128]{1,0:T(8,128)(2,1)} %a_ref.1) | copy-start | bytes 3145732
